TPU v7x, 128 devices: a whole 4x4x4 slice. The times are simulated.
128 devices in a mesh: row: 16 (over y_hi, x, core), col: 8 (over z, y_lo).
Axes of the slice: x: 4, y: 4 (y_hi: 2, y_lo: 2; y = y_hi * 2 + y_lo), z: 4, core: 2. Of those that a mesh axis runs over, the one named last changes fastest.
Arguments:
- residual: bfloat16 [16, 8, 2048, 512], P('row', 'col'), may hold values from -6 to 6
- self_tiles: bfloat16 [16, 8, 2048, 2048], P('row', 'col'), may hold values from -0.09375 to 0.09375
- side_tiles: bfloat16 [16, 8, 2048, 2048], P('row', 'col'), may hold values from -0.09375 to 0.09375
- row_cluster_basis: bfloat16 [16, 8, 2048, 32], P('row', 'col'), may hold values from -0.125 to 0.125
- column_cluster_basis: bfloat16 [16, 8, 2048, 32], P('row', 'col'), may hold values from -1 to 1
- couplings: bfloat16 [16, 8, 64, 32, 32], P('row', 'col'), may hold values from -0.1875 to 0.1875
- near_side: int32 [16, 8], P('row', 'col'), may hold values from -1 to 1
- adm_targets: int32 [16, 8, 64], P('row', 'col'), may hold values from 0 to 127, as said below
- adm_ranks: int32 [16, 8, 64], P('row', 'col'), may hold values from 8 to 32
- adm_count: int32 [16, 8], P('row', 'col'), may hold values from 1 to 64
Outputs:
- gradient: float32 [16, 8, 2048, 512], P('row', 'col')
Inputs may be any that keep to these rules, and one draw needn't show every extreme that they name: `near_side`: -1 or +1 names the cluster row before or after around the loop of 16 rows; 0 means no such tile. Each entry of adm_targets for the block row of linear index i is the linear index of a cluster other than i; slot 0 names i - 1 or i + 1, counted round the 128 clusters; targets may repeat.
All inputs are finite; a program needn't handle non-finite values.
Results may differ from a plain program's by a relative error of at most 0.0033.
Values may be sent and summed in bfloat16 or wider, within the bound.
A program may use at most 128 MiB of HBM per device.

v0:
```python
import jax
import jax.numpy as jnp
from jax import lax
from jax.sharding import Mesh
from jax.sharding import PartitionSpec as P

ROW = ("row_0", "row_1", "row_2")
COL = ("col_0", "col_1")
ROW_COL = ("row_0", "row_1", "row_2", "col_0", "col_1")


def with_halo(block, sides, width):
    for axis, dim in sides:
        count = lax.axis_size(axis)
        forward = [(i, i + 1) for i in range(count - 1)]
        forward.append((count - 1, 0))
        backward = [(target, source) for source, target in forward]
        low = lax.ppermute(
            lax.slice_in_dim(block, block.shape[dim] - width, None, axis=dim), axis, forward
        )
        high = lax.ppermute(lax.slice_in_dim(block, 0, width, axis=dim), axis, backward)
        block = jnp.concatenate([low, block, high], axis=dim)
    return block


def cut_rows(length, count):
    unit = 8 if length >= 8 * count else 1
    return [length // unit * k // count * unit for k in range(1, count)]


def all_blocks(value, axes, sequence):
    pieces = value[None]
    for k in sequence:
        pieces = lax.all_gather(pieces, axes[k], axis=0, tiled=True)
    held = [lax.axis_size(axes[k]) for k in reversed(sequence)]
    pieces = pieces.reshape(*held, *value.shape)
    turned = sorted(range(len(sequence)), key=lambda place: sequence[len(sequence) - 1 - place])
    return pieces.transpose(*turned, *range(len(sequence), pieces.ndim)).reshape(-1, *value.shape)


def in_order(pieces, dim):
    pieces = jnp.moveaxis(pieces, 0, dim)
    dims = pieces.shape
    return pieces.reshape(*dims[:dim], dims[dim] * dims[dim + 1], *dims[dim + 2 :])


def gather_at_once(value, axes, dim):
    split_at = max(range(max(1, value.ndim - 1)), key=lambda d: value.shape[d])
    count, done = (len(axes), [])
    for initial, slab in enumerate(
        jnp.split(value, cut_rows(value.shape[split_at], count), axis=split_at)
    ):
        if slab.size:
            sequence = [(initial - k) % count for k in range(count)]
            done.append(all_blocks(slab, axes, sequence))
    return in_order(jnp.concatenate(done, axis=split_at + 1), dim)


def contract(tile, values):
    return lax.dot_general(
        tile, values, (((0,), (0,)), ((), ())), preferred_element_type=jnp.float32
    )


def on_device(
    residual,
    self_tiles,
    side_tiles,
    row_cluster_basis,
    column_cluster_basis,
    couplings,
    near_side,
    adm_targets,
    adm_ranks,
    adm_count,
):
    slot_count = couplings.shape[2]
    rank_dimension = couplings.shape[3]
    cluster_groups = lax.axis_size(ROW) * lax.axis_size(COL)
    local_rows = residual[0, 0]
    coefficient_table = contract(row_cluster_basis[0, 0], local_rows).astype(jnp.bfloat16)
    rank_index = jnp.arange(rank_dimension, dtype=jnp.int32)
    slot_index = jnp.arange(slot_count, dtype=jnp.int32)
    keep_mask = (rank_index[None, :] < adm_ranks[0, 0][:, None]) & (slot_index < adm_count[0, 0])[
        :, None
    ]
    keep_float = keep_mask.astype(jnp.float32)
    masked = couplings[0, 0].astype(jnp.float32) * keep_float[:, :, None] * keep_float[:, None, :]
    onehot = (
        adm_targets[0, 0][:, None] == jnp.arange(cluster_groups, dtype=jnp.int32)[None, :]
    ).astype(jnp.float32)
    coupled_blocks = lax.dot_general(
        onehot,
        masked.reshape(slot_count, rank_dimension * rank_dimension),
        (((0,), (0,)), ((), ())),
        precision=lax.Precision.HIGHEST,
        preferred_element_type=jnp.float32,
    )
    coupled_blocks = coupled_blocks.reshape(cluster_groups, rank_dimension, rank_dimension)
    padded = with_halo(residual, ((ROW, 0),), 1)
    side_offset = near_side[0, 0]
    neighbour = lax.dynamic_index_in_dim(padded, side_offset + 1, 0, keepdims=False)[0]
    own_part = contract(self_tiles[0, 0], local_rows)
    side_part = contract(side_tiles[0, 0], neighbour) * (side_offset != 0).astype(jnp.float32)
    received = lax.all_to_all(
        coupled_blocks.astype(jnp.bfloat16), ROW_COL, split_axis=0, concat_axis=0, tiled=True
    ).astype(coupled_blocks.dtype)
    dual_sums = jnp.einsum(
        "cab,can->bn",
        received,
        gather_at_once(coefficient_table[None], ROW_COL, 0).astype(jnp.float32),
        precision=lax.Precision.HIGHEST,
    )
    dual_vector = dual_sums.astype(jnp.bfloat16)
    distant_part = jnp.dot(
        column_cluster_basis[0, 0], dual_vector, preferred_element_type=jnp.float32
    )
    gradient = own_part + side_part + distant_part
    return gradient[None, None]


def solution(mesh):
    torus = Mesh(mesh.devices.reshape(2, 4, 2, 4, 2), ("row_0", "row_1", "row_2", "col_0", "col_1"))
    in_specs = (
        P(ROW, COL, None, None),
        P(ROW, COL, None, None),
        P(ROW, COL, None, None),
        P(ROW, COL, None, None),
        P(ROW, COL, None, None),
        P(ROW, COL, None, None, None),
        P(ROW, COL),
        P(ROW, COL, None),
        P(ROW, COL, None),
        P(ROW, COL),
    )
    out_specs = P(ROW, COL, None, None)
    return jax.shard_map(
        on_device, mesh=torus, in_specs=in_specs, out_specs=out_specs, check_vma=False
    )
```

profile of v0, /device:TPU:1, one launch (start us, length us, event | category | flops | bytes accessed | tf_op | source)
XLA Modules:
  0.0 273.0 jit_solution(9813288460616339119)
XLA Ops:
  0.0 2.6 collective-permute-start
  3.3 0.7 fusion.37
  3.9 1.0 fusion.29
  4.9 1.1 convolution_convert_fusion
  6.0 1.4 copy.40
  7.5 1.5 reshape.163
  9.0 12.3 %all-to-all-start = ((bf16[128,2,512]{2,1,0:T(2,128)(2,1)}), bf16[128,2,512]{2,1,0:T(2,128)(2,1)}, u32[]{:S(2)}, u32[]{:S(2)}) async-start(bf16[128,2,512]{2,1,0:T(2,128)(2,1)} %reshape.163), calls=%async_computation | async-start | bytes 524288 | tf_op jit(solution)/shard_map/all_to_all | solution.py:105
  21.3 1.4 fusion.25
  22.7 9.9 %all-gather = bf16[2,6,512]{2,1,0:T(8,128)(2,1)S(1)} all-gather(bf16[1,6,512]{2,1,0:T(8,128)(2,1)S(1)} %get-tuple-element.9), channel_id=2, replica_groups=mesh['row_0'=2,'row_1'=4,'row_2'=2,'col_0'=4,'col_1'=2] {'row_0'}, dimensions={0}, use_global_device_ids=true | all-gather | bytes 18432 | tf_op jit(solution)/shard_map/all_gather | solution.py:34
  32.6 4.4 %all-gather.1 = bf16[4,6,512]{2,1,0:T(8,128)(2,1)S(1)} all-gather(bf16[2,6,512]{2,1,0:T(8,128)(2,1)S(1)} %all-gather), channel_id=3, replica_groups=mesh['row_0'=2,'row_1'=4,'row_2'=2,'col_0'=4,'col_1'=2] {'col_1'}, dimensions={0}, use_global_device_ids=true | all-gather | bytes 36864 | tf_op jit(solution)/shard_map/all_gather | solution.py:34
  37.0 9.9 %all-gather.2 = bf16[16,6,512]{2,1,0:T(8,128)(2,1)S(1)} all-gather(bf16[4,6,512]{2,1,0:T(8,128)(2,1)S(1)} %all-gather.1), channel_id=4, replica_groups=mesh['row_0'=2,'row_1'=4,'row_2'=2,'col_0'=4,'col_1'=2] {'col_0'}, dimensions={0}, use_global_device_ids=true | all-gather | bytes 122880 | tf_op jit(solution)/shard_map/all_gather | solution.py:34
  46.9 5.7 %all-gather.3 = bf16[32,6,512]{2,0,1:T(8,128)(2,1)S(1)} all-gather(bf16[16,6,512]{2,0,1:T(8,128)(2,1)S(1)} %copy.41), channel_id=5, replica_groups=mesh['row_0'=2,'row_1'=4,'row_2'=2,'col_0'=4,'col_1'=2] {'row_2'}, dimensions={0}, use_global_device_ids=true | all-gather | bytes 294912 | tf_op jit(solution)/shard_map/all_gather | solution.py:34
  52.6 15.9 %all-gather.4 = bf16[128,6,512]{2,0,1:T(8,128)(2,1)S(1)} all-gather(bf16[32,6,512]{2,0,1:T(8,128)(2,1)S(1)} %all-gather.3), channel_id=6, replica_groups=mesh['row_0'=2,'row_1'=4,'row_2'=2,'col_0'=4,'col_1'=2] {'row_1'}, dimensions={0}, use_global_device_ids=true | all-gather | bytes 983040 | tf_op jit(solution)/shard_map/all_gather | solution.py:34
  68.8 0.9 copy.63
  70.0 0.9 constant_dynamic-update-slice_fusion.3
  70.9 9.0 %all-gather.5 = bf16[4,6,512]{2,1,0:T(8,128)(2,1)S(1)} all-gather(bf16[1,6,512]{2,1,0:T(8,128)(2,1)S(1)} %get-tuple-element.8), channel_id=7, replica_groups=mesh['row_0'=2,'row_1'=4,'row_2'=2,'col_0'=4,'col_1'=2] {'row_1'}, dimensions={0}, use_global_device_ids=true | all-gather | bytes 30720 | tf_op jit(solution)/shard_map/all_gather | solution.py:34
  79.9 4.9 %all-gather.6 = bf16[8,6,512]{2,1,0:T(8,128)(2,1)S(1)} all-gather(bf16[4,6,512]{2,1,0:T(8,128)(2,1)S(1)} %all-gather.5), channel_id=8, replica_groups=mesh['row_0'=2,'row_1'=4,'row_2'=2,'col_0'=4,'col_1'=2] {'row_0'}, dimensions={0}, use_global_device_ids=true | all-gather | bytes 73728 | tf_op jit(solution)/shard_map/all_gather | solution.py:34
  84.9 3.6 %all-gather.7 = bf16[16,6,512]{2,0,1:T(8,128)(2,1)S(1)} all-gather(bf16[8,6,512]{2,0,1:T(8,128)(2,1)S(1)} %copy.43), channel_id=9, replica_groups=mesh['row_0'=2,'row_1'=4,'row_2'=2,'col_0'=4,'col_1'=2] {'col_1'}, dimensions={0}, use_global_device_ids=true | all-gather | bytes 147456 | tf_op jit(solution)/shard_map/all_gather | solution.py:34
  88.5 9.6 %all-gather.8 = bf16[64,6,512]{2,0,1:T(8,128)(2,1)S(1)} all-gather(bf16[16,6,512]{2,0,1:T(8,128)(2,1)S(1)} %all-gather.7), channel_id=10, replica_groups=mesh['row_0'=2,'row_1'=4,'row_2'=2,'col_0'=4,'col_1'=2] {'col_0'}, dimensions={0}, use_global_device_ids=true | all-gather | bytes 491520 | tf_op jit(solution)/shard_map/all_gather | solution.py:34
  98.1 12.4 %all-gather.9 = bf16[128,6,512]{2,0,1:T(8,128)(2,1)S(1)} all-gather(bf16[64,6,512]{2,0,1:T(8,128)(2,1)S(1)} %all-gather.8), channel_id=11, replica_groups=mesh['row_0'=2,'row_1'=4,'row_2'=2,'col_0'=4,'col_1'=2] {'row_2'}, dimensions={0}, use_global_device_ids=true | all-gather | bytes 1179648 | tf_op jit(solution)/shard_map/all_gather | solution.py:34
  110.7 0.8 copy.62
  111.8 1.8 all-gather.10
  113.6 9.4 %all-gather.11 = bf16[8,7,512]{2,1,0:T(8,128)(2,1)S(1)} all-gather(bf16[2,7,512]{2,1,0:T(8,128)(2,1)S(1)} %all-gather.10), channel_id=13, replica_groups=mesh['row_0'=2,'row_1'=4,'row_2'=2,'col_0'=4,'col_1'=2] {'row_1'}, dimensions={0}, use_global_device_ids=true | all-gather | bytes 71680 | tf_op jit(solution)/shard_map/all_gather | solution.py:34
  123.1 5.2 %all-gather.12 = bf16[16,7,512]{2,0,1:T(8,128)(2,1)S(1)} all-gather(bf16[8,7,512]{2,0,1:T(8,128)(2,1)S(1)} %copy.45), channel_id=14, replica_groups=mesh['row_0'=2,'row_1'=4,'row_2'=2,'col_0'=4,'col_1'=2] {'row_0'}, dimensions={0}, use_global_device_ids=true | all-gather | bytes 172032 | tf_op jit(solution)/shard_map/all_gather | solution.py:34
  128.3 4.3 %all-gather.13 = bf16[32,7,512]{2,0,1:T(8,128)(2,1)S(1)} all-gather(bf16[16,7,512]{2,0,1:T(8,128)(2,1)S(1)} %all-gather.12), channel_id=15, replica_groups=mesh['row_0'=2,'row_1'=4,'row_2'=2,'col_0'=4,'col_1'=2] {'col_1'}, dimensions={0}, use_global_device_ids=true | all-gather | bytes 344064 | tf_op jit(solution)/shard_map/all_gather | solution.py:34
  132.6 11.8 %all-gather.14 = bf16[128,7,512]{2,0,1:T(8,128)(2,1)S(1)} all-gather(bf16[32,7,512]{2,0,1:T(8,128)(2,1)S(1)} %all-gather.13), channel_id=16, replica_groups=mesh['row_0'=2,'row_1'=4,'row_2'=2,'col_0'=4,'col_1'=2] {'col_0'}, dimensions={0}, use_global_device_ids=true | all-gather | bytes 1146880 | tf_op jit(solution)/shard_map/all_gather | solution.py:34
  144.8 0.9 copy.60
  146.1 9.3 %all-gather.15 = bf16[4,6,512]{2,1,0:T(8,128)(2,1)S(1)} all-gather(bf16[1,6,512]{2,1,0:T(8,128)(2,1)S(1)} %get-tuple-element.7), channel_id=17, replica_groups=mesh['row_0'=2,'row_1'=4,'row_2'=2,'col_0'=4,'col_1'=2] {'col_0'}, dimensions={0}, use_global_device_ids=true | all-gather | bytes 30720 | tf_op jit(solution)/shard_map/all_gather | solution.py:34
  155.4 11.8 %all-gather.16 = bf16[8,6,512]{2,1,0:T(8,128)(2,1)S(1)} all-gather(bf16[4,6,512]{2,1,0:T(8,128)(2,1)S(1)} %all-gather.15), channel_id=18, replica_groups=mesh['row_0'=2,'row_1'=4,'row_2'=2,'col_0'=4,'col_1'=2] {'row_2'}, dimensions={0}, use_global_device_ids=true | all-gather | bytes 73728 | tf_op jit(solution)/shard_map/all_gather | solution.py:34
  167.2 9.3 %all-gather.17 = bf16[32,6,512]{2,0,1:T(8,128)(2,1)S(1)} all-gather(bf16[8,6,512]{2,0,1:T(8,128)(2,1)S(1)} %copy.47), channel_id=19, replica_groups=mesh['row_0'=2,'row_1'=4,'row_2'=2,'col_0'=4,'col_1'=2] {'row_1'}, dimensions={0}, use_global_device_ids=true | all-gather | bytes 245760 | tf_op jit(solution)/shard_map/all_gather | solution.py:34
  176.5 6.7 %all-gather.18 = bf16[64,6,512]{2,0,1:T(8,128)(2,1)S(1)} all-gather(bf16[32,6,512]{2,0,1:T(8,128)(2,1)S(1)} %all-gather.17), channel_id=20, replica_groups=mesh['row_0'=2,'row_1'=4,'row_2'=2,'col_0'=4,'col_1'=2] {'row_0'}, dimensions={0}, use_global_device_ids=true | all-gather | bytes 589824 | tf_op jit(solution)/shard_map/all_gather | solution.py:34
  183.2 7.3 %all-gather.19 = bf16[128,6,512]{2,0,1:T(8,128)(2,1)S(1)} all-gather(bf16[64,6,512]{2,0,1:T(8,128)(2,1)S(1)} %all-gather.18), channel_id=21, replica_groups=mesh['row_0'=2,'row_1'=4,'row_2'=2,'col_0'=4,'col_1'=2] {'col_1'}, dimensions={0}, use_global_device_ids=true | all-gather | bytes 1179648 | tf_op jit(solution)/shard_map/all_gather | solution.py:34
  190.7 1.1 copy.61
  192.1 3.5 %all-gather.20 = bf16[2,7,512]{2,1,0:T(8,128)(2,1)S(1)} all-gather(bf16[1,7,512]{2,1,0:T(8,128)(2,1)S(1)} %get-tuple-element.5), channel_id=22, replica_groups=mesh['row_0'=2,'row_1'=4,'row_2'=2,'col_0'=4,'col_1'=2] {'col_1'}, dimensions={0}, use_global_device_ids=true | all-gather | bytes 21504 | tf_op jit(solution)/shard_map/all_gather | solution.py:34
  195.6 9.0 %all-gather.21 = bf16[8,7,512]{2,1,0:T(8,128)(2,1)S(1)} all-gather(bf16[2,7,512]{2,1,0:T(8,128)(2,1)S(1)} %all-gather.20), channel_id=23, replica_groups=mesh['row_0'=2,'row_1'=4,'row_2'=2,'col_0'=4,'col_1'=2] {'col_0'}, dimensions={0}, use_global_device_ids=true | all-gather | bytes 71680 | tf_op jit(solution)/shard_map/all_gather | solution.py:34
  204.6 10.8 %all-gather.22 = bf16[16,7,512]{2,0,1:T(8,128)(2,1)S(1)} all-gather(bf16[8,7,512]{2,0,1:T(8,128)(2,1)S(1)} %copy.49), channel_id=24, replica_groups=mesh['row_0'=2,'row_1'=4,'row_2'=2,'col_0'=4,'col_1'=2] {'row_2'}, dimensions={0}, use_global_device_ids=true | all-gather | bytes 172032 | tf_op jit(solution)/shard_map/all_gather | solution.py:34
  215.4 11.1 %all-gather.23 = bf16[64,7,512]{2,0,1:T(8,128)(2,1)S(1)} all-gather(bf16[16,7,512]{2,0,1:T(8,128)(2,1)S(1)} %all-gather.22), channel_id=25, replica_groups=mesh['row_0'=2,'row_1'=4,'row_2'=2,'col_0'=4,'col_1'=2] {'row_1'}, dimensions={0}, use_global_device_ids=true | all-gather | bytes 573440 | tf_op jit(solution)/shard_map/all_gather | solution.py:34
  226.5 12.5 %all-gather.24 = bf16[128,7,512]{2,0,1:T(8,128)(2,1)S(1)} all-gather(bf16[64,7,512]{2,0,1:T(8,128)(2,1)S(1)} %all-gather.23), channel_id=26, replica_groups=mesh['row_0'=2,'row_1'=4,'row_2'=2,'col_0'=4,'col_1'=2] {'row_0'}, dimensions={0}, use_global_device_ids=true | all-gather | bytes 1376256 | tf_op jit(solution)/shard_map/all_gather | solution.py:34
  239.7 0.9 constant_dynamic-update-slice_fusion.2
  240.6 1.0 constant_dynamic-update-slice_fusion.1
  241.6 0.9 constant_dynamic-update-slice_fusion
  242.5 10.5 %fusion.2 = f32[2048,512]{1,0:T(8,128)} fusion(bf16[1,1,2048,2048]{3,2,1,0:T(8,128)(2,1)} %param.11, bf16[1,1,2048,512]{3,2,1,0:T(8,128)(2,1)} %param.10), kind=kOutput, calls=%fused_computation.2 | convolution fusion | flops 4294967296 | bytes 14680064 | tf_op jit(solution)/shard_map/dot_general | solution.py:60
  253.0 1.0 bitcast_dynamic-update-slice_fusion
  254.0 1.9 reshape.164
  255.9 3.1 %fusion.19 = bf16[32,512]{1,0:T(8,128)(2,1)S(1)} fusion(bf16[128,1,32,512]{3,0,2,1:T(8,128)(2,1)} %bitcast_dynamic-update-slice_fusion, bf16[128,32,32]{2,1,0:T(8,128)(2,1)S(1)} %reshape.164), kind=kOutput, calls=%fused_computation.20 | convolution fusion | flops 134234112 | bytes 4489216 | tf_op jit(solution)/shard_map/cab,can->bn/dot_general | solution.py:108
  259.1 0.7 fusion.30
  259.8 0.8 copy-done.2
  260.7 12.3 %fusion.4 = f32[1,1,2048,512]{3,2,1,0:T(8,128)} fusion(f32[512,2048]{0,1:T(8,128)S(1)} %fusion.30, f32[2048,512]{1,0:T(8,128)} %fusion.2, bf16[1,1,2048,2048]{3,2,1,0:T(8,128)(2,1)} %param.12, s32[]{:T(128)S(6)} %select_n.4, bf16[1,1,2048,512]{3,2,1,0:T(8,128)(2,1)} %collective-permute-done, bf16[1,1,2048,512]{3,2,1,0:T(8,128)(2,1)S(1)} %copy-done.2, ...), kind=kOutput, calls=%fused_computation.8 | convolution fusion | flops 4300210176 | bytes 27262984 | tf_op jit(solution)/shard_map/dot_general | solution.py:60
  (25 shorter events, 2.4 us)
Async XLA Ops:
  0.0 259.1 %copy-start = (bf16[1,1,2048,32]{2,3,1,0:T(8,128)(2,1)S(1)}, bf16[1,1,2048,32]{2,3,1,0:T(8,128)(2,1)}, u32[]{:S(2)}) copy-start(bf16[1,1,2048,32]{2,3,1,0:T(8,128)(2,1)} %param.14) | copy-start | bytes 393220
  0.0 21.3 %copy-start.1 = (bf16[1,1,2048,512]{3,2,1,0:T(8,128)(2,1)S(1)}, bf16[1,1,2048,512]{3,2,1,0:T(8,128)(2,1)}, u32[]{:S(2)}) copy-start(bf16[1,1,2048,512]{3,2,1,0:T(8,128)(2,1)} %param.10) | copy-start | bytes 6291460
  0.0 259.8 %collective-permute-start = (bf16[1,1,2048,512]{3,2,1,0:T(8,128)(2,1)}, bf16[1,1,2048,512]{3,2,1,0:T(8,128)(2,1)}, u32[]{:S(2)}, u32[]{:S(2)}) collective-permute-start(bf16[1,1,2048,512]{3,2,1,0:T(8,128)(2,1)} %param.10), channel_id=1, source_target_pairs={{0,8},{8,16},{16,24},{24,32},{32,40},{40,48},{48,56},{56,64},{64,7... | collective-permute-start | bytes 6291464 | tf_op jit(solution)/shard_map/ppermute | solution.py:18
  2.6 257.2 %collective-permute-start.1 = (bf16[1,1,2048,512]{3,2,1,0:T(8,128)(2,1)}, bf16[1,1,2048,512]{3,2,1,0:T(8,128)(2,1)}, u32[]{:S(2)}, u32[]{:S(2)}) collective-permute-start(bf16[1,1,2048,512]{3,2,1,0:T(8,128)(2,1)} %param.10), channel_id=1, source_target_pairs={{8,0},{16,8},{24,16},{32,24},{40,32},{48,40},{56,48},{64,56},{72,6... | collective-permute-start | bytes 6291464 | tf_op jit(solution)/shard_map/ppermute | solution.py:21
  9.0 245.0 %all-to-all-start = ((bf16[128,2,512]{2,1,0:T(2,128)(2,1)}), bf16[128,2,512]{2,1,0:T(2,128)(2,1)}, u32[]{:S(2)}, u32[]{:S(2)}) async-start(bf16[128,2,512]{2,1,0:T(2,128)(2,1)} %reshape.163), calls=%async_computation | async-start | bytes 524288 | tf_op jit(solution)/shard_map/all_to_all | solution.py:105
  259.1 1.6 copy-start.2
where the time goes:
time: 275 us; the launch traced here: 273 us
  blocking collectives  209 us (76%)
  matrix products  29.1 us (11%)
  local copies, waits for them, and re-layouts  16.6 us (6%)
  starting transfers between devices  14.8 us (5%)
    all_gather x25, blocking collectives, all_blocks(): pieces = lax.all_gather(pieces, axes[k], axis=0, tiled=True)  209 us
    dot_general x3, matrix products, contract(): lax.dot_general(tile, values, (((0,), (0,)), ((), ())), preferred_element...  24.2 us
    all_to_all x1, starting transfers between devices, on_device(): lax.all_to_all(coupled_blocks.astype(jnp.bfloat16), ROW_COL, split_axis=0...  12.3 us
    unnamed x12, local copies, waits for them, and re-layouts  8.06 us
  transfers between devices with their start and end apart: 3, of which 0 were waited for; matrix products, arithmetic and copies ran while one was open for 13% of the time, Pallas kernels for 0%

commit v1 on v0

v1 whole, which is shorter than its diff:
```python
import jax
import jax.numpy as jnp
from jax import lax
from jax.experimental import pallas as pl
from jax.experimental.pallas import tpu as pltpu
from jax.sharding import PartitionSpec as P

MESH = pl.DeviceIdType.MESH
LEAF, K, NRHS, ADM = 2048, 32, 512, 64
CHUNKS = 16
ROWS = LEAF // CHUNKS
WINDOW = 3
BF, F32 = jnp.bfloat16, jnp.float32


def tdot(a, b):
    return lax.dot_general(a, b, (((0,), (0,)), ((), ())), preferred_element_type=F32)


def kernel(
    res, selft, sidet, rowb, colb, coup, side, targ, rank, count, out,
    res_v, self_v, side_v, rowb_v, colb_v, coup_v, side_s, targ_v, rank_v, count_v, nb_on, nb_off, nbs, acc,
    d32, dsend, m_v, g_v, pf, psend, r_v, fsend, f_v,
    lsem, osem, on_s, on_r, off_s, off_r, xp_s, xp_r, z_s, z_r, c_s, c_r, m_s, m_r, y_s, y_r, f_s, f_r,
):
    p, q = lax.axis_index("row"), lax.axis_index("col")
    c, x, z = p % 2, (p // 2) % 4, q // 2
    y = (p // 8) * 2 + q % 2
    xp, h = x % 2, x // 2

    def dev(x_, y_, z_, c_):
        return ((y_ // 2) * 8 + x_ * 2 + c_, z_ * 2 + y_ % 2)

    def load(k, src, dst):
        return pltpu.make_async_copy(src, dst, lsem.at[k])

    loads = [
        load(0, res, res_v), load(1, rowb, rowb_v), load(2, coup, coup_v),
        load(3, selft, self_v), load(4, sidet, side_v), load(5, colb, colb_v),
        load(6, side, side_s), load(7, targ, targ_v), load(8, rank, rank_v), load(9, count, count_v),
    ]
    for cp in loads:
        cp.start()

    group = []
    for k in range(1, 16):
        dc, dz, dx = k // 8, (k // 2) % 4, k % 2
        c2, x2 = (c + dc) % 2, (xp + dx) % 2
        z_to, z_from = (z + dz) % 4, (z + 4 - dz) % 4
        group.append((k, dev(2 * h + x2, y, z_to, c2), c2 * 8 + z_to * 2 + x2, c2 * 8 + z_from * 2 + x2))
    off_dev = ((p + 15 + 2 * c) % 16, q)
    on_dev = (p + 1 - 2 * c, q)
    y_devs = [dev(x, (y + k) % 4, z, c) for k in (1, 2, 3)]
    far_dev = dev(3 - x, y, z, c)
    bar = pltpu.get_barrier_semaphore()
    partners = [g[1] for g in group] + [off_dev, far_dev] + y_devs
    for d in partners:
        pl.semaphore_signal(bar, 1, device_id=d, device_id_type=MESH)

    me = c * 8 + z * 2 + xp
    loads[0].wait()
    loads[1].wait()
    g_v[me] = jnp.dot(rowb_v[...], res_v[...], preferred_element_type=F32).astype(BF)

    def rdma(src, dst, s, r, d):
        return pltpu.make_async_remote_copy(
            src_ref=src, dst_ref=dst, send_sem=s, recv_sem=r, device_id=d, device_id_type=MESH
        )

    def off(k):
        rows = pl.ds(k * ROWS, ROWS)
        return rdma(res_v.at[rows], nb_off.at[rows], off_s.at[k], off_r.at[k], off_dev)

    def pump(k):
        if k < CHUNKS:
            if k >= WINDOW:
                off(k - WINDOW).wait_send()
            off(k).start()

    on = rdma(res_v, nb_on, on_s, on_r, on_dev)
    xp_copy = rdma(g_v.at[me], g_v.at[me], xp_s, xp_r, dev(4 * h + 1 - x, y, z, c))

    pl.semaphore_wait(bar, len(partners))
    xp_copy.start()
    for k in range(WINDOW):
        pump(k)
    on.start()

    for cp in loads[6:]:
        cp.wait()
    loads[2].wait()
    rank_row = rank_v[0:1, :]
    r = lax.broadcasted_iota(jnp.int32, (128, ADM), 0)
    s_i = lax.broadcasted_iota(jnp.int32, (128, ADM), 1)
    t, d = r // 16, r % 16
    y2, nf = t // 2, t % 2
    c2, z2, x2 = d // 8, (d // 2) % 4, 2 * h + d % 2
    x3 = jnp.where(nf == 0, x2, 3 - x2)
    j = ((y2 // 2) * 8 + x3 * 2 + c2) * 8 + z2 * 2 + y2 % 2
    hit = jnp.where((targ_v[0:1, :] == j) & (s_i < count_v[0:1, 0:1]), rank_row, 0)
    mask_b = (r % K < rank_row).astype(F32)
    lane16 = lax.broadcasted_iota(jnp.int32, (16, 128), 1)

    def dense(a, _):
        lhs = jnp.where(hit > a, 1.0, 0.0).astype(BF)
        block = coup_v[pl.ds(pl.multiple_of(a * K, K), K), :].astype(F32)
        rhs = (jnp.concatenate([block] * 4, axis=0) * mask_b).astype(BF)
        full = lax.dot_general(lhs, rhs, (((1,), (1,)), ((), ())), preferred_element_type=F32)
        for u in range(2):
            got = jnp.zeros((16, 128), F32)
            for i in range(4):
                got = jnp.where(lane16 // K == i, full[(4 * u + i) * 16:(4 * u + i + 1) * 16, :], got)
            d32[u, pl.ds(a, 16, stride=K), :] = got
        return 0

    lax.fori_loop(0, K, dense, 0)
    for u in range(2):
        dsend[:, :, u * 128:(u + 1) * 128] = d32[u].reshape(16, K, 128).astype(BF)
    m_v[me] = dsend[me]
    m_copies = [rdma(dsend.at[to], m_v.at[me], m_s.at[k - 1], m_r.at[k - 1], d_) for k, d_, to, _ in group]
    for cp in m_copies:
        cp.start()
    pump(3)
    pump(4)

    xp_copy.wait_recv()
    mine = pl.ds(c * 8 + z * 2, 2)
    z_copies = [
        rdma(g_v.at[mine], g_v.at[mine], z_s.at[k - 1], z_r.at[k - 1], dev(x, y, (z + k) % 4, c)) for k in (1, 2, 3)
    ]
    for cp in z_copies:
        cp.start()
    pump(5)

    loads[3].wait()

    def self_part(i, _):
        cols = pl.ds(pl.multiple_of(i * 256, 256), 256)
        acc[cols, :] = tdot(self_v[:, cols], res_v[...])
        return 0

    lax.fori_loop(0, 4, self_part, 0)
    pump(6)
    for cp in z_copies:
        cp.wait_recv()
    half = pl.ds(c * 8, 8)
    c_copy = rdma(g_v.at[half], g_v.at[half], c_s, c_r, on_dev)
    c_copy.start()
    for cp in m_copies:
        cp.wait_recv()
    c_copy.wait_recv()
    pf[...] = tdot(m_v[...].reshape(512, 256), g_v[...].reshape(512, NRHS))
    psend[...] = pf[...].reshape(4, 2 * K, NRHS).astype(BF)
    y_copies = [
        rdma(psend.at[(y + k) % 4], r_v.at[y], y_s.at[k - 1], y_r.at[k - 1], y_devs[k - 1]) for k in (1, 2, 3)
    ]
    for cp in y_copies:
        cp.start()
    pump(7)
    lax.fori_loop(4, 8, self_part, 0)
    pump(8)

    near = side_s[0:1, 0:1]
    w_on = jnp.broadcast_to(jnp.where(near == 1 - 2 * c, 1.0, 0.0), (1, NRHS)).astype(BF)
    w_off = jnp.broadcast_to(jnp.where(near == 2 * c - 1, 1.0, 0.0), (1, NRHS)).astype(BF)
    on.wait_recv()
    loads[4].wait()

    def side_group(g):
        off(2 * g).wait_recv()
        off(2 * g + 1).wait_recv()
        rows = pl.ds(g * 256, 256)
        nbs[...] = nb_on[rows, :] * w_on + nb_off[rows, :] * w_off

    def side_tile(g, i):
        cols = pl.ds(pl.multiple_of(i * 512, 512), 512)
        acc[cols, :] += tdot(side_v[pl.ds(g * 256, 256), cols], nbs[...])

    def side_part(g):
        side_group(g)

        def body(i, _):
            side_tile(g, i)
            return 0

        lax.fori_loop(0, 4, body, 0)

    side_part(0)
    pump(9)
    side_part(1)
    pump(10)
    side_part(2)
    pump(11)
    pump(12)

    for cp in y_copies:
        cp.wait_recv()
    total = pf[pl.ds(pl.multiple_of(y * 2 * K, 2 * K), 2 * K), :]
    for k in (1, 2, 3):
        total = total + r_v[(y + k) % 4].astype(F32)
    pf[0:2 * K, :] = total
    fsend[...] = total[K:, :].astype(BF)
    far = rdma(fsend, f_v, f_s, f_r, far_dev)
    far.start()
    side_part(3)
    pump(13)
    pump(14)
    far.wait_recv()
    loads[5].wait()
    dual = (pf[0:K, :] + f_v[...].astype(F32)).astype(BF)

    def distant(i, _):
        rows = pl.ds(pl.multiple_of(i * 512, 512), 512)
        acc[rows, :] += tdot(colb_v[:, rows], dual)
        return 0

    lax.fori_loop(0, 4, distant, 0)
    side_part(4)
    pump(15)
    side_part(5)
    side_part(6)
    side_group(7)

    def put(i):
        rows = pl.ds(pl.multiple_of(i * 512, 512), 512)
        return pltpu.make_async_copy(acc.at[rows], out.at[rows], osem.at[i])

    def last(i, _):
        side_tile(7, i)
        put(i).start()
        return 0

    lax.fori_loop(0, 4, last, 0)
    for k in range(CHUNKS - WINDOW, CHUNKS):
        off(k).wait_send()
    for cp in [on, xp_copy, c_copy, far] + z_copies + m_copies + y_copies:
        cp.wait_send()
    for i in range(4):
        put(i).wait()


def on_device(*args):
    res, selft, sidet, rowb, colb, coup, side, targ, rank, count = args
    anyspace = pl.BlockSpec(memory_space=pl.ANY)
    dma = pltpu.SemaphoreType.DMA
    out = pl.pallas_call(
        kernel,
        out_shape=jax.ShapeDtypeStruct((LEAF, NRHS), F32),
        in_specs=[anyspace] * 10,
        out_specs=anyspace,
        scratch_shapes=[
            pltpu.VMEM((LEAF, NRHS), BF),
            pltpu.VMEM((LEAF, LEAF), BF),
            pltpu.VMEM((LEAF, LEAF), BF),
            pltpu.VMEM((K, LEAF), BF),
            pltpu.VMEM((K, LEAF), BF),
            pltpu.VMEM((K * K, ADM), BF),
            pltpu.VMEM((1, 1), jnp.int32),
            pltpu.VMEM((1, ADM), jnp.int32),
            pltpu.VMEM((1, ADM), jnp.int32),
            pltpu.VMEM((1, 1), jnp.int32),
            pltpu.VMEM((LEAF, NRHS), BF),
            pltpu.VMEM((LEAF, NRHS), BF),
            pltpu.VMEM((256, NRHS), BF),
            pltpu.VMEM((LEAF, NRHS), F32),
            pltpu.VMEM((2, 16 * K, 128), F32),
            pltpu.VMEM((16, K, 256), BF),
            pltpu.VMEM((16, K, 256), BF),
            pltpu.VMEM((16, K, NRHS), BF),
            pltpu.VMEM((256, NRHS), F32),
            pltpu.VMEM((4, 2 * K, NRHS), BF),
            pltpu.VMEM((4, 2 * K, NRHS), BF),
            pltpu.VMEM((K, NRHS), BF),
            pltpu.VMEM((K, NRHS), BF),
            dma((10,)), dma((4,)), dma, dma, dma((CHUNKS,)), dma((CHUNKS,)), dma, dma,
            dma((3,)), dma((3,)), dma, dma, dma((15,)), dma((15,)), dma((3,)), dma((3,)), dma, dma,
        ],
        compiler_params=pltpu.CompilerParams(
            collective_id=0, has_side_effects=True, vmem_limit_bytes=63 * 2**20
        ),
    )(
        res[0, 0], selft[0, 0], sidet[0, 0], rowb[0, 0].T, colb[0, 0].T,
        coup[0, 0].transpose(1, 2, 0).reshape(K * K, ADM),
        side, targ[0], rank[0], count,
    )
    return out[None, None]


def solution(mesh):
    rc = ("row", "col")
    in_specs = tuple(P(*rc, *[None] * n) for n in (2, 2, 2, 2, 2, 3, 0, 1, 1, 0))
    return jax.shard_map(
        on_device, mesh=mesh, in_specs=in_specs, out_specs=P(*rc, None, None), check_vma=False
    )
```

time: 275 us -> 62.3 us (0.23)
  the two profiles are of different devices: /device:TPU:1 before, /device:TPU:7 now
where the time goes in v1:
time: 62.3 us; the launch traced here: 62.1 us
  Pallas kernels  56.2 us (90%)
  local copies, waits for them, and re-layouts  4.64 us (7%)
  between operations  1.3 us (2%)
    pallas_call x1, Pallas kernels, on_device(): pl.pallas_call(kernel, out_shape=jax.ShapeDtypeStruct((LEAF, NRHS), F32),...  56.2 us
    unnamed x1, local copies, waits for them, and re-layouts  4.64 us

profile of v1, /device:TPU:7, one launch (start us, length us, event | category | flops | bytes accessed | tf_op | source)
XLA Modules:
  0.0 62.1 jit_solution(8057383599299912394)
XLA Ops:
  1.3 56.2 %shard_map.100 = f32[2048,512]{1,0:T(8,128)} custom-call(bf16[2048,512]{1,0:T(8,128)(2,1)} %bitcast.20, bf16[2048,2048]{1,0:T(8,128)(2,1)} %bitcast.18, bf16[2048,2048]{1,0:T(8,128)(2,1)} %bitcast.19, bf16[32,2048]{1,0:T(8,128)(2,1)} %bitcast.22, bf16[32,2048]{1,0:T(8,128)(2,1)} %bitcast.23, bf16[1024,64]{1,0:T(8,128)(2,1)} %bitcast.21, ...), custom_call_target="tpu_custom_call" | custom-call | tf_op jit(solution)/shard_map/pallas_call | solution.py:246
  57.5 4.6 %copy.14 = f32[1,1,2048,512]{3,2,1,0:T(8,128)} copy(f32[1,1,2048,512]{3,2,1,0:T(8,128)} %bitcast.17) | data formatting | bytes 8388608

commit v2 on v0

v2 whole, which is shorter than its diff:
```python
import jax
import jax.numpy as jnp
from jax import lax
from jax.experimental import pallas as pl
from jax.experimental.pallas import tpu as pltpu
from jax.sharding import PartitionSpec as P

MESH = pl.DeviceIdType.MESH
LEAF, K, NRHS, ADM = 2048, 32, 512, 64
HALF = NRHS // 2
BF, F32 = jnp.bfloat16, jnp.float32
PIECES = [(0, i * 512, 512) for i in range(4)] + [(1, i * 512, 512) for i in range(3)] + [(1, 1536, 256), (1, 1792, 256)]
LAST = 256


def tdot(a, b):
    return lax.dot_general(a, b, (((0,), (0,)), ((), ())), preferred_element_type=F32)


def scope(name):
    return jax.named_scope(name)


def kernel(
    res, selft, sidet, rowb, colb, coup, targ, rank, side, count,
    acc, side_v, nbl, colb_v, dual,
    res_v, self_v, rowb_v, coup_v, targ_v, rank_v, side_s, count_v, nb_on, nb_off,
    targ_r, raw_s, raw_r, d32, dsend, m_v, g_v, pf, psend, r_v, qs, f_v, n_v,
    lsem, on_s, on_r, off_s, off_r, xp_s, xp_r, z_s, z_r, c_s, c_r, m_s, m_r, y_s, y_r, f_s, f_r, n_s, n_r, w_s, w_r,
):
    p, q = lax.axis_index("row"), lax.axis_index("col")
    c, x, z = p % 2, (p // 2) % 4, q // 2
    y = (p // 8) * 2 + q % 2
    xp, h = x % 2, x // 2
    hx = 1 + h
    handler = x == hx
    near_core = hx % 2

    def dev(x_, y_, z_, c_):
        return ((y_ // 2) * 8 + x_ * 2 + c_, z_ * 2 + y_ % 2)

    off_dev = ((p + 15 + 2 * c) % 16, q)
    on_dev = (p + 1 - 2 * c, q)
    y_devs = [dev(x, (y + k) % 4, z, c) for k in (1, 2, 3)]
    side_x = 4 * h + 1 - x
    far_devs = [dev(2 - 2 * h + k // 2, y, z, k % 2) for k in range(4)]
    outer_dev = dev(hx, y, z, c)
    bar = pltpu.get_barrier_semaphore()
    common = [off_dev, dev(side_x, y, z, 0), dev(side_x, y, z, 1)]
    peers = [dev(x, y, (z + k % 4) % 4, (c + k // 4) % 2) for k in range(1, 8)]
    inner = common + far_devs + y_devs + peers
    outer = common + [on_dev] + [dev(2 - h, y, z, 0), dev(2 - h, y, z, 1)]

    @pl.when(handler)
    def _():
        for d in inner:
            pl.semaphore_signal(bar, 1, device_id=d, device_id_type=MESH)

    @pl.when(jnp.logical_not(handler))
    def _():
        for d in outer:
            pl.semaphore_signal(bar, 1, device_id=d, device_id_type=MESH)

    def load(k, src, dst):
        return pltpu.make_async_copy(src, dst, lsem.at[k])

    loads = [
        load(0, res.at[:, :HALF], res_v.at[0]), load(1, res.at[:, HALF:], res_v.at[1]), load(2, rowb, rowb_v),
        load(3, coup, coup_v), load(4, targ, targ_v), load(5, rank, rank_v), load(6, count, count_v),
        load(7, selft, self_v), load(8, sidet, side_v), load(9, colb, colb_v), load(10, side, side_s),
    ]
    for k in (3, 4, 5, 6, 2, 0, 1, 10, 7, 8, 9):
        loads[k].start()

    with scope("A_wload"):
        for cp in loads[3:7]:
            cp.wait()
    r = lax.broadcasted_iota(jnp.int32, (K * K, ADM), 0)
    s_i = lax.broadcasted_iota(jnp.int32, (K * K, ADM), 1)
    live = (jnp.maximum(r // K, r % K) < rank_v[0:1, :]) & (s_i < count_v[0:1, 0:1])
    masked = jnp.where(live, coup_v[...].astype(F32), 0.0)
    raw_s[...] = jnp.concatenate([masked[:512], masked[512:]], axis=1).astype(BF)

    lane = lax.broadcasted_iota(jnp.int32, (8, 128), 1)

    def densify(raw, targets, slot):
        r = lax.broadcasted_iota(jnp.int32, (256, 128), 0)
        at = lax.broadcasted_iota(jnp.int32, (256, 128), 1) // ADM == r // 128
        t, d = (r // 8) % 16, r % 8
        c2, z2 = d // 4, d % 4
        x3 = jnp.where(c2 == near_core, 2 * h, 2 - 2 * h) + (t // 2) % 2
        y2, ct = t // 4, t % 2
        j = ((y2 // 2) * 8 + x3 * 2 + ct) * 8 + z2 * 2 + y2 % 2
        row = targets[0:1, :]
        hit = jnp.where((jnp.concatenate([row, row], axis=1) == j) & at, 1.0, 0.0).astype(BF)

        def body(a, _):
            block = raw[pl.ds(pl.multiple_of(a * K, K), K), :]
            full = lax.dot_general(
                hit, jnp.concatenate([block] * 4, axis=0), (((1,), (1,)), ((), ())), preferred_element_type=F32
            )
            for v in range(2):
                for u in range(4):
                    got = jnp.zeros((8, 128), F32)
                    for i in range(4):
                        at = (16 * v + 4 * u + i) * 8
                        got = jnp.where(lane // K == i, full[at:at + 8, :], got)
                    d32[u, pl.ds(a + 16 * v, 8, stride=K), :] = got
            return 0

        lax.fori_loop(0, 16, body, 0, unroll=4)
        for u in range(4):
            dsend[slot, :, :, u * 128:(u + 1) * 128] = d32[u].reshape(8, K, 128).astype(BF)

    @pl.when(handler)
    def _():
        with scope("B_dense"):
            densify(raw_s, targ_v, 0)

    me = c * 8 + z * 2 + xp
    mate = c * 8 + z * 2 + 1 - xp

    with scope("C_coef"):
        for k in (2, 0, 1):
            loads[k].wait()
        for u in range(2):
            g_v[me, :, u * HALF:(u + 1) * HALF] = jnp.dot(
                rowb_v[...], res_v[u], preferred_element_type=F32
            ).astype(BF)

    def rdma(src, dst, s, r, d):
        return pltpu.make_async_remote_copy(
            src_ref=src, dst_ref=dst, send_sem=s, recv_sem=r, device_id=d, device_id_type=MESH
        )

    def off(k):
        u, r0, n = PIECES[k]
        rows = pl.ds(r0, n)
        return rdma(res_v.at[u, rows], nb_off.at[u, rows], off_s.at[k], off_r.at[k], off_dev)

    offs = [off(k) for k in range(len(PIECES))]
    on = rdma(res_v, nb_on, on_s, on_r, on_dev)
    xp_copy = rdma(g_v.at[me], g_v.at[me], xp_s, xp_r, outer_dev)
    raw_copy = rdma(raw_s, raw_r, w_s.at[0], w_r.at[0], outer_dev)
    targ_copy = rdma(targ_v, targ_r, w_s.at[1], w_r.at[1], outer_dev)
    m_copies = []
    for i, src in enumerate((me, mate)):
        for k in range(1, 8):
            c2, z2 = (c + k // 4) % 2, (z + k) % 4
            m_copies.append(
                rdma(dsend.at[i, c2 * 4 + z2], m_v.at[src], m_s.at[i, k], m_r.at[i, k], dev(hx, y, z2, c2))
            )

    with scope("D_bar"):
        @pl.when(handler)
        def _():
            pl.semaphore_wait(bar, len(inner))

        @pl.when(jnp.logical_not(handler))
        def _():
            pl.semaphore_wait(bar, len(outer))


    @pl.when(handler)
    def _():
        for cp in m_copies[:7]:
            cp.start()
        m_v[me] = dsend[0, c * 4 + z]

    @pl.when(jnp.logical_not(handler))
    def _():
        for cp in (xp_copy, targ_copy, raw_copy):
            cp.start()

    for cp in offs:
        cp.start()
    on.start()

    def self_part(i, _):
        cols = pl.ds(pl.multiple_of(i * 256, 256), 256)
        got = tdot(self_v[:, cols], jnp.concatenate([res_v[0], res_v[1]], axis=1))
        acc[0, cols, :] = got[:, :HALF]
        acc[1, cols, :] = got[:, HALF:]
        return 0

    with scope("E_wself"):
        loads[7].wait()
    mine = pl.ds(c * 8 + z * 2, 2)
    z_copies = [
        rdma(g_v.at[mine], g_v.at[mine], z_s.at[k - 1], z_r.at[k - 1], dev(x, y, (z + k) % 4, c)) for k in (1, 2, 3)
    ]
    half = pl.ds(c * 8, 8)
    c_copy = rdma(g_v.at[half], g_v.at[half], c_s, c_r, on_dev)
    y_copies = [
        rdma(psend.at[(y + k) % 4], r_v.at[y], y_s.at[k - 1], y_r.at[k - 1], y_devs[k - 1]) for k in (1, 2, 3)
    ]
    near_is_me = c == near_core
    far = [rdma(qs.at[k], f_v, f_s.at[k], f_r, far_devs[k]) for k in range(4)]
    near = [rdma(qs.at[xp * 2 + 1 - c], n_v, n_s.at[0], n_r, on_dev)] + [
        rdma(qs.at[(1 - xp) * 2 + k], n_v, n_s.at[1 + k], n_r, dev(side_x, y, z, k)) for k in (0, 1)
    ]

    with scope("E_self1"):
        lax.fori_loop(0, 3, self_part, 0, unroll=3)

    @pl.when(handler)
    def _():
        with scope("F_wxp"):
            xp_copy.wait_recv()
        for cp in z_copies:
            cp.start()
        with scope("F_wraw"):
            targ_copy.wait_recv()
            raw_copy.wait_recv()
        with scope("F_dense"):
            densify(raw_r, targ_r, 1)
        for cp in m_copies[7:]:
            cp.start()
        m_v[mate] = dsend[1, c * 4 + z]

    with scope("F_self2"):
        lax.fori_loop(3, 6, self_part, 0, unroll=3)

    @pl.when(handler)
    def _():
        with scope("H_wz"):
            for cp in z_copies:
                cp.wait_recv()
        c_copy.start()

    with scope("H_self3"):
        lax.fori_loop(6, 8, self_part, 0, unroll=2)

    @pl.when(handler)
    def _():
        with scope("I_wm"):
            for cp in m_copies:
                cp.wait_recv()
        with scope("I_wc"):
            c_copy.wait_recv()
        with scope("I_pf"):
            pf[...] = tdot(m_v[...].reshape(512, 512), g_v[...].reshape(512, NRHS))
            psend[...] = pf[...].reshape(4, 4 * K, NRHS).astype(BF)
        for cp in y_copies:
            cp.start()

    loads[10].wait()
    which = side_s[0:1, 0:1]
    w_on = jnp.broadcast_to(jnp.where(which == 1 - 2 * c, 1.0, 0.0), (1, HALF)).astype(BF)
    w_off = jnp.broadcast_to(jnp.where(which == 2 * c - 1, 1.0, 0.0), (1, HALF)).astype(BF)
    with scope("G_won"):
        on.wait_recv()
        loads[8].wait()

    def picked(k):
        u, r0, n = PIECES[k]
        rows = pl.ds(r0, n)
        with scope(f"w{k}"):
            offs[k].wait_recv()
        return nb_on[u, rows, :] * w_on + nb_off[u, rows, :] * w_off

    def side_part(k):
        u, r0, n = PIECES[k]
        nbl[pl.ds(0, n), :] = picked(k)
        with scope(f"S{k}"):
            def body(i, _):
                cols = pl.ds(pl.multiple_of(i * 512, 512), 512)
                acc[u, cols, :] += tdot(side_v[pl.ds(r0, n), cols], nbl[pl.ds(0, n), :])
                return 0

            lax.fori_loop(0, 4, body, 0, unroll=4)

    side_part(0)
    side_part(1)
    side_part(2)
    side_part(3)

    @pl.when(handler)
    def _():
        with scope("K_wy"):
            for cp in y_copies:
                cp.wait_recv()
        total = pf[pl.ds(pl.multiple_of(y * 4 * K, 4 * K), 4 * K), :]
        for k in (1, 2, 3):
            total = total + r_v[(y + k) % 4].astype(F32)
        qs[...] = total.astype(BF).reshape(4, K, NRHS)

        @pl.when(near_is_me)
        def _():
            for cp in near:
                cp.start()
            n_v[...] = qs[xp * 2 + c]

        @pl.when(jnp.logical_not(near_is_me))
        def _():
            for cp in far:
                cp.start()

    side_part(4)
    side_part(5)
    side_part(6)
    side_part(7)
    with scope("Q_sends"):
        for cp in offs + [on]:
            cp.wait_send()

        @pl.when(handler)
        def _():
            for cp in m_copies + z_copies + [c_copy] + y_copies:
                cp.wait_send()

            @pl.when(near_is_me)
            def _():
                for cp in near:
                    cp.wait_send()

            @pl.when(jnp.logical_not(near_is_me))
            def _():
                for cp in far:
                    cp.wait_send()

        @pl.when(jnp.logical_not(handler))
        def _():
            for cp in (xp_copy, targ_copy, raw_copy):
                cp.wait_send()

    nbl[pl.ds(0, LAST), :] = picked(8)
    with scope("M_wdual"):
        far[0].wait_recv()

        @pl.when(jnp.logical_not(handler & near_is_me))
        def _():
            near[0].wait_recv()

    loads[9].wait()
    dual[...] = (n_v[...].astype(F32) + f_v[...].astype(F32)).astype(BF)


def finish(acc, side_v, nbl, colb_v, dual, out, tmp, sem):
    copies = []
    for u in range(2):
        for i in range(4):
            rows = pl.ds(i * 512, 512)
            got = acc[u, rows, :] + tdot(colb_v[:, rows], dual[:, u * HALF:(u + 1) * HALF])
            if u:
                got = got + tdot(side_v[pl.ds(LEAF - LAST, LAST), rows], nbl[pl.ds(0, LAST), :])
            tmp[u, rows, :] = got
            cp = pltpu.make_async_copy(tmp.at[u, rows], out.at[rows, pl.ds(u * HALF, HALF)], sem.at[u * 4 + i])
            cp.start()
            copies.append(cp)
    for cp in copies:
        cp.wait()


def on_device(*args):
    res, selft, sidet, rowb, colb, coup, side, targ, rank, count = args
    anyspace = pl.BlockSpec(memory_space=pl.ANY)
    vm = pl.BlockSpec(memory_space=pltpu.VMEM)
    hbm = pl.BlockSpec(memory_space=pltpu.HBM)
    dma = pltpu.SemaphoreType.DMA
    n = len(PIECES)
    ins = (
        res[0, 0], selft[0, 0], sidet[0, 0], rowb[0, 0].T, colb[0, 0].T,
        coup[0, 0].transpose(1, 2, 0).reshape(K * K, ADM), targ[0], rank[0], side, count,
    )
    ins = [a if a.size == 1 else pltpu.with_memory_space_constraint(a, pltpu.HBM) for a in ins]
    mid = pl.pallas_call(
        kernel,
        out_shape=[
            pltpu.VMEM((2, LEAF, HALF), F32), pltpu.VMEM((LEAF, LEAF), BF), pltpu.VMEM((512, HALF), BF),
            pltpu.VMEM((K, LEAF), BF), pltpu.VMEM((K, NRHS), BF),
        ],
        in_specs=[hbm] * 8 + [anyspace] * 2,
        out_specs=[vm] * 5,
        scratch_shapes=[
            pltpu.VMEM((2, LEAF, HALF), BF),
            pltpu.VMEM((LEAF, LEAF), BF),
            pltpu.VMEM((K, LEAF), BF),
            pltpu.VMEM((K * K, ADM), BF),
            pltpu.VMEM((1, ADM), jnp.int32),
            pltpu.VMEM((1, ADM), jnp.int32),
            pltpu.VMEM((1, 1), jnp.int32),
            pltpu.VMEM((1, 1), jnp.int32),
            pltpu.VMEM((2, LEAF, HALF), BF),
            pltpu.VMEM((2, LEAF, HALF), BF),
            pltpu.VMEM((1, ADM), jnp.int32),
            pltpu.VMEM((512, 128), BF),
            pltpu.VMEM((512, 128), BF),
            pltpu.VMEM((4, 8 * K, 128), F32),
            pltpu.VMEM((2, 8, K, 512), BF),
            pltpu.VMEM((16, K, 512), BF),
            pltpu.VMEM((16, K, NRHS), BF),
            pltpu.VMEM((512, NRHS), F32),
            pltpu.VMEM((4, 4 * K, NRHS), BF),
            pltpu.VMEM((4, 4 * K, NRHS), BF),
            pltpu.VMEM((4, K, NRHS), BF),
            pltpu.VMEM((K, NRHS), BF),
            pltpu.VMEM((K, NRHS), BF),
            dma((11,)), dma, dma, dma((n,)), dma((n,)), dma, dma, dma((3,)), dma((3,)), dma, dma,
            dma((2, 8)), dma((2, 8)), dma((3,)), dma((3,)), dma((4,)), dma, dma((3,)), dma, dma((2,)), dma((2,)),
        ],
        compiler_params=pltpu.CompilerParams(
            collective_id=0, has_side_effects=True, vmem_limit_bytes=36 * 2**20
        ),
    )(*ins)
    out = pl.pallas_call(
        finish,
        out_shape=jax.ShapeDtypeStruct((LEAF, NRHS), F32),
        in_specs=[vm] * 5,
        out_specs=anyspace,
        scratch_shapes=[pltpu.VMEM((2, LEAF, HALF), F32), dma((8,))],
        compiler_params=pltpu.CompilerParams(vmem_limit_bytes=12 * 2**20),
    )(*mid)
    return out[None, None]


def solution(mesh):
    rc = ("row", "col")
    in_specs = tuple(P(*rc, *[None] * n) for n in (2, 2, 2, 2, 2, 3, 0, 1, 1, 0))
    return jax.shard_map(
        on_device, mesh=mesh, in_specs=in_specs, out_specs=P(*rc, None, None), check_vma=False
    )
```

time: 275 us -> 37.4 us (0.14)
  blocking collectives: 209 us -> 0 us
  Pallas kernels: 0 us -> 35.8 us
  matrix products: 29.1 us -> 0 us
  local copies, waits for them, and re-layouts: 16.6 us -> 0 us
  starting transfers between devices: 14.8 us -> 0 us
    all_gather x25 -> x0, blocking collectives: 209 us -> none  [all_blocks(): pieces = lax.all_gather(pieces, axes[k], axis=0, tiled=True)]
    pallas_call x0 -> x2, Pallas kernels: none -> 35.8 us  [the longest x1 33.4 us: on_device(): pl.pallas_call(kernel, out_shape=[pltpu.VMEM((2, LEAF, HALF), F32), pltpu...]
    dot_general x6 -> x0, matrix products: 29.1 us -> none  [the longest x3 24.2 us: contract(): lax.dot_general(tile, values, (((0,), (0,)), ((), ())), preferred_element...]
    all_to_all x1 -> x0, starting transfers between devices: 12.3 us -> none  [on_device(): lax.all_to_all(coupled_blocks.astype(jnp.bfloat16), ROW_COL, split_axis=0...]
    unnamed x12 -> x0, local copies, waits for them, and re-layouts: 8.06 us -> none
    reshape x12 -> x0, local copies, waits for them, and re-layouts: 5.94 us -> none  [the longest x8 4.69 us: all_blocks(): pieces = pieces.reshape(*held, *value.shape)]
  transfers between devices with their start and end apart: 3 -> 0, of which waited for: 0 -> 0; matrix products, arithmetic and copies ran while one was open for 13% -> 0% of each run, Pallas kernels for 0% -> 0%
where the time goes in v2:
time: 37.4 us; the launch traced here: 37.3 us
  Pallas kernels  35.8 us (96%)
  between operations  1.47 us (4%)
    pallas_call x1, Pallas kernels, on_device(): pl.pallas_call(kernel, out_shape=[pltpu.VMEM((2, LEAF, HALF), F32), pltpu...  33.4 us
    pallas_call x1, Pallas kernels, on_device(): pl.pallas_call(finish, out_shape=jax.ShapeDtypeStruct((LEAF, NRHS), F32),...  2.44 us

profile of v2, /device:TPU:1, one launch (start us, length us, event | category | flops | bytes accessed | tf_op | source)
XLA Modules:
  0.0 37.3 jit_solution(10423024941899852163)
XLA Ops:
  1.3 33.4 %shard_map.100 = (f32[2,2048,256]{2,1,0:T(8,128)S(1)}, bf16[2048,2048]{1,0:T(8,128)(2,1)S(1)}, bf16[512,256]{1,0:T(8,128)(2,1)S(1)}, bf16[32,2048]{1,0:T(8,128)(2,1)S(1)}, bf16[32,512]{1,0:T(8,128)(2,1)S(1)}) custom-call(bf16[2048,512]{1,0:T(8,128)(2,1)} %bitcast.19, bf16[2048,2048]{1,0:T(8,128)(2,1)} %bitcast.17, bf16[2048,2048]{1,0:T(8,128)(2,1)} %bitcast.18, ...), custom_call_target="tpu_custom_call" | custom-call | tf_op jit(solution)/shard_map/pallas_call | solution.py:367
  34.7 2.4 %shard_map.101 = f32[2048,512]{1,0:T(8,128)} custom-call(f32[2,2048,256]{2,1,0:T(8,128)S(1)} %get-tuple-element.10.acc, bf16[2048,2048]{1,0:T(8,128)(2,1)S(1)} %get-tuple-element.11.side_v, bf16[512,256]{1,0:T(8,128)(2,1)S(1)} %get-tuple-element.12.nbl, bf16[32,2048]{1,0:T(8,128)(2,1)S(1)} %get-tuple-element.13.colb_v, ...), custom_call_target="tpu_custom_call" | custom-call | tf_op jit(solution)/shard_map/pallas_call | solution.py:406

commit v3 on v2

v3 whole, which is shorter than its diff:
```python
import jax
import jax.numpy as jnp
from jax import lax
from jax.experimental import pallas as pl
from jax.experimental.pallas import tpu as pltpu
from jax.sharding import PartitionSpec as P

MESH = pl.DeviceIdType.MESH
LEAF, K, NRHS, ADM = 2048, 32, 512, 64
HALF = NRHS // 2
BF, F32 = jnp.bfloat16, jnp.float32
PIECES = [(0, i * 512, 512) for i in range(4)] + [(1, i * 512, 512) for i in range(3)] + [(1, 1536, 256), (1, 1792, 256)]
LAST = 256


def tdot(a, b):
    return lax.dot_general(a, b, (((0,), (0,)), ((), ())), preferred_element_type=F32)


def scope(name):
    return jax.named_scope(name)


def kernel(
    res, selft, sidet, rowb, colb, coup, targ, rank, side, count,
    acc, side_v, nbl, colb_v, dual,
    res_v, self_v, rowb_v, coup_v, targ_v, rank_v, side_s, count_v, nb_on, nb_off,
    targ_r, raw_s, raw_r, d32, ds_a, ds_b, m_a, m_b, g_v, p32, p2, ps, q_v, r_v, qs, f_v, n_v,
    lsem, ssem, off_r, on_r, xp_r, w_r, z_r, c_r, m_r, q_r, y_r, f_r, n_r,
):
    p, q = lax.axis_index("row"), lax.axis_index("col")
    c, x, z = p % 2, (p // 2) % 4, q // 2
    y = (p // 8) * 2 + q % 2
    xp, h = x % 2, x // 2
    hx = 1 + h
    handler = x == hx
    near_core = hx % 2

    def dev(x_, y_, z_, c_):
        return ((y_ // 2) * 8 + x_ * 2 + c_, z_ * 2 + y_ % 2)

    off_dev = ((p + 15 + 2 * c) % 16, q)
    on_dev = (p + 1 - 2 * c, q)
    y_devs = [dev(x, (y + k) % 4, z, c) for k in (1, 2, 3)]
    side_x = 4 * h + 1 - x
    far_devs = [dev(2 - 2 * h + k // 2, y, z, k % 2) for k in range(4)]
    outer_dev = dev(hx, y, z, c)
    bar = pltpu.get_barrier_semaphore()
    common = [off_dev, dev(side_x, y, z, 0), dev(side_x, y, z, 1)]
    peers = [dev(x, y, (z + k % 4) % 4, (c + k // 4) % 2) for k in range(1, 8)]
    inner = common + far_devs + y_devs + peers
    outer = common + [on_dev] + [dev(2 - h, y, z, 0), dev(2 - h, y, z, 1)]

    @pl.when(handler)
    def _():
        for d in inner:
            pl.semaphore_signal(bar, 1, device_id=d, device_id_type=MESH)

    @pl.when(jnp.logical_not(handler))
    def _():
        for d in outer:
            pl.semaphore_signal(bar, 1, device_id=d, device_id_type=MESH)

    def load(k, src, dst):
        return pltpu.make_async_copy(src, dst, lsem.at[k])

    def done(ref, sem):
        pltpu.make_async_copy(ref, ref, sem).wait()

    small = [load(0, coup, coup_v), load(1, targ, targ_v), load(2, rank, rank_v), load(3, count, count_v), load(4, side, side_s)]
    load_rowb = load(5, rowb, rowb_v)
    first = [load_rowb, load(6, res.at[:, :HALF], res_v.at[0]), load(6, res.at[:, HALF:], res_v.at[1])]
    load_self, load_side, load_colb = load(7, selft, self_v), load(8, sidet, side_v), load(9, colb, colb_v)
    for cp in first + small + [load_self]:
        cp.start()

    with scope("A_wload"):
        for cp in small:
            cp.wait()
    r = lax.broadcasted_iota(jnp.int32, (K * K, ADM), 0)
    s_i = lax.broadcasted_iota(jnp.int32, (K * K, ADM), 1)
    live = (jnp.maximum(r // K, r % K) < rank_v[0:1, :]) & (s_i < count_v[0:1, 0:1])
    masked = jnp.where(live, coup_v[...].astype(F32), 0.0)
    raw_s[...] = jnp.concatenate([masked[:512], masked[512:]], axis=1).astype(BF)

    lane = lax.broadcasted_iota(jnp.int32, (8, 128), 1)

    def densify(raw, targets, slot, ready=None):
        r = lax.broadcasted_iota(jnp.int32, (256, 128), 0)
        at = lax.broadcasted_iota(jnp.int32, (256, 128), 1) // ADM == r // 128
        t, d = (r // 8) % 16, r % 8
        c2, z2 = d // 4, d % 4
        x3 = jnp.where(c2 == near_core, 2 * h, 2 - 2 * h) + (t // 2) % 2
        kk, ct = t // 4, t % 2
        y2 = (y + jnp.where(kk == 0, 2, jnp.where(kk == 1, 1, jnp.where(kk == 2, 3, 0)))) % 4
        j = ((y2 // 2) * 8 + x3 * 2 + ct) * 8 + z2 * 2 + y2 % 2
        row = targets[0:1, :]
        hit = jnp.where((jnp.concatenate([row, row], axis=1) == j) & at, 1.0, 0.0).astype(BF)

        def body(a, _):
            block = raw[pl.ds(pl.multiple_of(a * K, K), K), :]
            full = lax.dot_general(
                hit, jnp.concatenate([block] * 4, axis=0), (((1,), (1,)), ((), ())), preferred_element_type=F32
            )
            for v in range(2):
                for u in range(4):
                    got = jnp.zeros((8, 128), F32)
                    for i in range(4):
                        at = (16 * v + 4 * u + i) * 8
                        got = jnp.where(lane // K == i, full[at:at + 8, :], got)
                    d32[u, pl.ds(a + 16 * v, 8, stride=K), :] = got
            return 0

        lax.fori_loop(0, 8, body, 0, unroll=4)
        if ready is not None:
            ready()
        lax.fori_loop(8, 16, body, 0, unroll=4)
        ds_a[slot] = d32[0].reshape(8, K, 128).astype(BF)
        for u in range(3):
            ds_b[slot, :, :, u * 128:(u + 1) * 128] = d32[1 + u].reshape(8, K, 128).astype(BF)

    mine, mate = c * 8 + z, c * 8 + 4 + z
    me = jnp.where(handler, mine, mate)

    with scope("C_coef"):
        load_rowb.wait()
        done(res_v, lsem.at[6])
        for u in range(2):
            g_v[me, :, u * HALF:(u + 1) * HALF] = jnp.dot(
                rowb_v[...], res_v[u], preferred_element_type=F32
            ).astype(BF)

    def rdma(src, dst, s, r, d):
        return pltpu.make_async_remote_copy(
            src_ref=src, dst_ref=dst, send_sem=s, recv_sem=r, device_id=d, device_id_type=MESH
        )

    def off(k):
        u, r0, n = PIECES[k]
        rows = pl.ds(r0, n)
        return rdma(res_v.at[u, rows], nb_off.at[u, rows], ssem.at[0], off_r.at[k], off_dev)

    offs = [off(k) for k in range(len(PIECES))]
    on = rdma(res_v, nb_on, ssem.at[7], on_r, on_dev)
    xp_copy = rdma(g_v.at[me], g_v.at[me], ssem.at[8], xp_r, outer_dev)
    raw_copies = [
        rdma(raw_s.at[pl.ds(i * 256, 256)], raw_r.at[pl.ds(i * 256, 256)], ssem.at[1], w_r.at[i], outer_dev) for i in (0, 1)
    ]
    targ_copy = rdma(targ_v, targ_r, ssem.at[9], w_r.at[2], outer_dev)
    m_copies = []
    for i, src in enumerate((mine, mate)):
        for l, (ds, m) in enumerate(((ds_a, m_a), (ds_b, m_b))):
            m_copies.append([
                rdma(
                    ds.at[i, (c + k // 4) % 2 * 4 + (z + k) % 4], m.at[src], ssem.at[2], m_r.at[l],
                    dev(hx, y, (z + k) % 4, (c + k // 4) % 2),
                ) for k in range(1, 8)
            ])
    z_copies = [
        [
            rdma(g_v.at[src], g_v.at[src], ssem.at[3], z_r.at[i], dev(x, y, (z + k) % 4, c))
            for k in (2, 1, 3)
        ] for i, src in enumerate((mine, mate))
    ]
    c_copies = []
    for i in range(2):
        part = pl.ds(c * 8 + 4 * i, 4)
        c_copies.append(rdma(g_v.at[part], g_v.at[part], ssem.at[4], c_r.at[i], on_dev))

    with scope("D_bar"):
        @pl.when(handler)
        def _():
            pl.semaphore_wait(bar, len(inner))

        @pl.when(jnp.logical_not(handler))
        def _():
            pl.semaphore_wait(bar, len(outer))


    @pl.when(handler)
    def _():
        for cp in z_copies[0]:
            cp.start()

    @pl.when(jnp.logical_not(handler))
    def _():
        for cp in [targ_copy] + raw_copies + [xp_copy]:
            cp.start()

    for cp in offs:
        cp.start()
    on.start()
    load_side.start()
    load_colb.start()

    @pl.when(handler)
    def _():
        with scope("B_dense"):
            densify(raw_s, targ_v, 0)
        for cp in m_copies[0] + m_copies[1]:
            cp.start()
        m_a[mine] = ds_a[0, c * 4 + z]
        m_b[mine] = ds_b[0, c * 4 + z]

    def self_part(i, _):
        cols = pl.ds(pl.multiple_of(i * 256, 256), 256)
        got = tdot(self_v[:, cols], jnp.concatenate([res_v[0], res_v[1]], axis=1))
        acc[0, cols, :] = got[:, :HALF]
        acc[1, cols, :] = got[:, HALF:]
        return 0

    with scope("E_wself"):
        load_self.wait()
    q_copies = [rdma(p2.at[k], q_v.at[k], ssem.at[5], q_r, y_devs[2 * k]) for k in (0, 1)]
    y_copies = [rdma(ps.at[k], r_v.at[k], ssem.at[5], y_r, y_devs[2 * k]) for k in (0, 1)]
    near_is_me = c == near_core
    far = [rdma(qs.at[k], f_v, ssem.at[6], f_r, far_devs[k]) for k in range(4)]
    near = [rdma(qs.at[xp * 2 + 1 - c], n_v, ssem.at[6], n_r, on_dev)] + [
        rdma(qs.at[(1 - xp) * 2 + k], n_v, ssem.at[6], n_r, dev(side_x, y, z, k)) for k in (0, 1)
    ]

    with scope("E_self1"):
        lax.fori_loop(0, 3, self_part, 0, unroll=3)

    @pl.when(handler)
    def _():
        with scope("F_wraw"):
            targ_copy.wait_recv()
            raw_copies[0].wait_recv()
        with scope("F_dense"):
            densify(raw_r, targ_r, 1, raw_copies[1].wait_recv)
        for cp in m_copies[2]:
            cp.start()
        with scope("F_wxp"):
            xp_copy.wait_recv()
        for cp in z_copies[1] + m_copies[3]:
            cp.start()
        m_a[mate] = ds_a[1, c * 4 + z]
        m_b[mate] = ds_b[1, c * 4 + z]
        with scope("F_wz"):
            done(g_v.at[pl.ds(0, 3)], z_r.at[0])
        c_copies[0].start()

    with scope("F_self2"):
        lax.fori_loop(3, 8, self_part, 0, unroll=5)

    @pl.when(handler)
    def _():
        with scope("H_wz"):
            done(g_v.at[pl.ds(0, 3)], z_r.at[1])
        c_copies[1].start()
        with scope("I_wma"):
            done(m_a.at[pl.ds(0, 14)], m_r.at[0])
        with scope("I_wc"):
            for cp in c_copies:
                cp.wait_recv()
        with scope("I_pa"):
            got = tdot(m_a[...].reshape(512, 128), g_v[...].reshape(512, NRHS)).astype(BF)
            p2[0] = got[:, :HALF]
            p2[1] = got[:, HALF:]
        for cp in q_copies:
            cp.start()
        with scope("I_wmb"):
            done(m_b.at[pl.ds(0, 14)], m_r.at[1])
        with scope("I_pb"):
            p32[...] = tdot(m_b[...].reshape(512, 384), g_v[...].reshape(512, NRHS)).reshape(3, 128, NRHS)

    which = side_s[0:1, 0:1]
    w_on = jnp.broadcast_to(jnp.where(which == 1 - 2 * c, 1.0, 0.0), (1, HALF)).astype(BF)
    w_off = jnp.broadcast_to(jnp.where(which == 2 * c - 1, 1.0, 0.0), (1, HALF)).astype(BF)
    with scope("G_won"):
        on.wait_recv()
        load_side.wait()

    def picked(k):
        u, r0, n = PIECES[k]
        rows = pl.ds(r0, n)
        with scope(f"w{k}"):
            offs[k].wait_recv()
        return nb_on[u, rows, :] * w_on + nb_off[u, rows, :] * w_off

    def side_part(k):
        u, r0, n = PIECES[k]
        nbl[pl.ds(0, n), :] = picked(k)
        with scope(f"S{k}"):
            def body(i, _):
                cols = pl.ds(pl.multiple_of(i * 512, 512), 512)
                acc[u, cols, :] += tdot(side_v[pl.ds(r0, n), cols], nbl[pl.ds(0, n), :])
                return 0

            lax.fori_loop(0, 4, body, 0, unroll=4)

    side_part(0)
    side_part(1)

    @pl.when(handler)
    def _():
        with scope("J_wq"):
            done(q_v, q_r)
        for k in range(2):
            cols = slice(k * HALF, (k + 1) * HALF)
            rest = slice((1 - k) * HALF, (2 - k) * HALF)
            ps[k, :, cols] = (p32[k, :, cols] + q_v[k].astype(F32)).astype(BF)
            ps[k, :, rest] = p32[k, :, rest].astype(BF)
            y_copies[k].start()

    side_part(2)
    side_part(3)

    @pl.when(handler)
    def _():
        with scope("K_wy"):
            done(r_v, y_r)
        total = p32[2] + r_v[0].astype(F32) + r_v[1].astype(F32)
        qs[...] = total.astype(BF).reshape(4, K, NRHS)

        @pl.when(near_is_me)
        def _():
            for cp in near:
                cp.start()
            n_v[...] = qs[xp * 2 + c]

        @pl.when(jnp.logical_not(near_is_me))
        def _():
            for cp in far:
                cp.start()

    side_part(4)
    side_part(5)
    side_part(6)
    side_part(7)
    with scope("Q_sends"):
        done(res_v, ssem.at[0])
        on.wait_send()

        @pl.when(handler)
        def _():
            done(g_v.at[pl.ds(0, 14)], ssem.at[2])
            done(g_v.at[pl.ds(0, 6)], ssem.at[3])
            done(g_v.at[pl.ds(0, 8)], ssem.at[4])
            done(g_v.at[pl.ds(0, 12)], ssem.at[5])

            @pl.when(near_is_me)
            def _():
                done(g_v.at[pl.ds(0, 3)], ssem.at[6])

            @pl.when(jnp.logical_not(near_is_me))
            def _():
                done(g_v.at[pl.ds(0, 4)], ssem.at[6])

        @pl.when(jnp.logical_not(handler))
        def _():
            done(raw_s, ssem.at[1])
            xp_copy.wait_send()
            targ_copy.wait_send()

    nbl[pl.ds(0, LAST), :] = picked(8)
    with scope("M_wfar"):
        far[0].wait_recv()

    with scope("M_wdual"):
        @pl.when(jnp.logical_not(handler & near_is_me))
        def _():
            near[0].wait_recv()

    load_colb.wait()
    dual[...] = (n_v[...].astype(F32) + f_v[...].astype(F32)).astype(BF)


def finish(acc, side_v, nbl, colb_v, dual, out, tmp, sem):
    for i in range(8):
        rows = pl.ds(i * 256, 256)
        for u in range(2):
            got = acc[u, rows, :] + tdot(colb_v[:, rows], dual[:, u * HALF:(u + 1) * HALF])
            if u:
                got = got + tdot(side_v[pl.ds(LEAF - LAST, LAST), rows], nbl[pl.ds(0, LAST), :])
            tmp[rows, u * HALF:(u + 1) * HALF] = got
        pltpu.make_async_copy(tmp.at[rows], out.at[rows], sem).start()
    pltpu.make_async_copy(tmp, out, sem).wait()


def on_device(*args):
    res, selft, sidet, rowb, colb, coup, side, targ, rank, count = args
    anyspace = pl.BlockSpec(memory_space=pl.ANY)
    vm = pl.BlockSpec(memory_space=pltpu.VMEM)
    hbm = pl.BlockSpec(memory_space=pltpu.HBM)
    dma = pltpu.SemaphoreType.DMA
    n = len(PIECES)
    ins = (
        res[0, 0], selft[0, 0], sidet[0, 0], rowb[0, 0].T, colb[0, 0].T,
        coup[0, 0].transpose(1, 2, 0).reshape(K * K, ADM), targ[0], rank[0], side, count,
    )
    ins = [a if a.size == 1 else pltpu.with_memory_space_constraint(a, pltpu.HBM) for a in ins]
    mid = pl.pallas_call(
        kernel,
        out_shape=[
            pltpu.VMEM((2, LEAF, HALF), F32), pltpu.VMEM((LEAF, LEAF), BF), pltpu.VMEM((512, HALF), BF),
            pltpu.VMEM((K, LEAF), BF), pltpu.VMEM((K, NRHS), BF),
        ],
        in_specs=[hbm] * 8 + [anyspace] * 2,
        out_specs=[vm] * 5,
        scratch_shapes=[
            pltpu.VMEM((2, LEAF, HALF), BF),
            pltpu.VMEM((LEAF, LEAF), BF),
            pltpu.VMEM((K, LEAF), BF),
            pltpu.VMEM((K * K, ADM), BF),
            pltpu.VMEM((1, ADM), jnp.int32),
            pltpu.VMEM((1, ADM), jnp.int32),
            pltpu.VMEM((1, 1), jnp.int32),
            pltpu.VMEM((1, 1), jnp.int32),
            pltpu.VMEM((2, LEAF, HALF), BF),
            pltpu.VMEM((2, LEAF, HALF), BF),
            pltpu.VMEM((1, ADM), jnp.int32),
            pltpu.VMEM((512, 128), BF),
            pltpu.VMEM((512, 128), BF),
            pltpu.VMEM((4, 8 * K, 128), F32),
            pltpu.VMEM((2, 8, K, 128), BF),
            pltpu.VMEM((2, 8, K, 384), BF),
            pltpu.VMEM((16, K, 128), BF),
            pltpu.VMEM((16, K, 384), BF),
            pltpu.VMEM((16, K, NRHS), BF),
            pltpu.VMEM((3, 128, NRHS), F32),
            pltpu.VMEM((2, 128, HALF), BF),
            pltpu.VMEM((2, 128, NRHS), BF),
            pltpu.VMEM((2, 128, HALF), BF),
            pltpu.VMEM((2, 128, NRHS), BF),
            pltpu.VMEM((4, K, NRHS), BF),
            pltpu.VMEM((K, NRHS), BF),
            pltpu.VMEM((K, NRHS), BF),
            dma((10,)), dma((10,)), dma((n,)), dma, dma, dma((3,)), dma((2,)), dma((2,)), dma((2,)), dma, dma, dma, dma,
        ],
        compiler_params=pltpu.CompilerParams(
            collective_id=0, has_side_effects=True, vmem_limit_bytes=36 * 2**20
        ),
    )(*ins)
    out = pl.pallas_call(
        finish,
        out_shape=jax.ShapeDtypeStruct((LEAF, NRHS), F32),
        in_specs=[vm] * 5,
        out_specs=anyspace,
        scratch_shapes=[pltpu.VMEM((LEAF, NRHS), F32), dma],
        compiler_params=pltpu.CompilerParams(vmem_limit_bytes=12 * 2**20),
    )(*mid)
    return out[None, None]


def solution(mesh):
    rc = ("row", "col")
    in_specs = tuple(P(*rc, *[None] * n) for n in (2, 2, 2, 2, 2, 3, 0, 1, 1, 0))
    return jax.shard_map(
        on_device, mesh=mesh, in_specs=in_specs, out_specs=P(*rc, None, None), check_vma=False
    )
```

time: 37.4 us -> 36.8 us (0.984)
  Pallas kernels: 35.8 us -> 35.2 us
    pallas_call x1, Pallas kernels: 33.4 us -> 32.8 us  [on_device(): pl.pallas_call(kernel, out_shape=[pltpu.VMEM((2, LEAF, HALF), F32), pltpu...]
where the time goes in v3:
time: 36.8 us; the launch traced here: 36.7 us
  Pallas kernels  35.2 us (96%)
  between operations  1.47 us (4%)
    pallas_call x1, Pallas kernels, on_device(): pl.pallas_call(kernel, out_shape=[pltpu.VMEM((2, LEAF, HALF), F32), pltpu...  32.8 us
    pallas_call x1, Pallas kernels, on_device(): pl.pallas_call(finish, out_shape=jax.ShapeDtypeStruct((LEAF, NRHS), F32),...  2.46 us

profile of v3, /device:TPU:1, one launch (start us, length us, event | category | flops | bytes accessed | tf_op | source)
XLA Modules:
  0.0 36.7 jit_solution(17181384670369977115)
XLA Ops:
  1.3 32.8 %shard_map.100 = (f32[2,2048,256]{2,1,0:T(8,128)S(1)}, bf16[2048,2048]{1,0:T(8,128)(2,1)S(1)}, bf16[512,256]{1,0:T(8,128)(2,1)S(1)}, bf16[32,2048]{1,0:T(8,128)(2,1)S(1)}, bf16[32,512]{1,0:T(8,128)(2,1)S(1)}) custom-call(bf16[2048,512]{1,0:T(8,128)(2,1)} %bitcast.19, bf16[2048,2048]{1,0:T(8,128)(2,1)} %bitcast.17, bf16[2048,2048]{1,0:T(8,128)(2,1)} %bitcast.18, ...), custom_call_target="tpu_custom_call" | custom-call | tf_op jit(solution)/shard_map/pallas_call | solution.py:394
  34.1 2.5 %shard_map.101 = f32[2048,512]{1,0:T(8,128)} custom-call(f32[2,2048,256]{2,1,0:T(8,128)S(1)} %get-tuple-element.10.acc, bf16[2048,2048]{1,0:T(8,128)(2,1)S(1)} %get-tuple-element.11.side_v, bf16[512,256]{1,0:T(8,128)(2,1)S(1)} %get-tuple-element.12.nbl, bf16[32,2048]{1,0:T(8,128)(2,1)S(1)} %get-tuple-element.13.colb_v, ...), custom_call_target="tpu_custom_call" | custom-call | tf_op jit(solution)/shard_map/pallas_call | solution.py:436

commit v4 on v3

--- a/solution.py
+++ b/solution.py
@@ -9,8 +9,8 @@
 LEAF, K, NRHS, ADM = 2048, 32, 512, 64
 HALF = NRHS // 2
 BF, F32 = jnp.bfloat16, jnp.float32
-PIECES = [(0, i * 512, 512) for i in range(4)] + [(1, i * 512, 512) for i in range(3)] + [(1, 1536, 256), (1, 1792, 256)]
-LAST = 256
+PIECES = [(0, i * 512, 512) for i in range(4)] + [(1, i * 512, 512) for i in range(3)] + [(1, 1536, 288), (1, 1824, 224)]
+LAST = 224
 
 
 def tdot(a, b):
@@ -111,10 +111,10 @@
                     d32[u, pl.ds(a + 16 * v, 8, stride=K), :] = got
             return 0
 
-        lax.fori_loop(0, 8, body, 0, unroll=4)
+        lax.fori_loop(0, 8, body, 0, unroll=8)
         if ready is not None:
             ready()
-        lax.fori_loop(8, 16, body, 0, unroll=4)
+        lax.fori_loop(8, 16, body, 0, unroll=8)
         ds_a[slot] = d32[0].reshape(8, K, 128).astype(BF)
         for u in range(3):
             ds_b[slot, :, :, u * 128:(u + 1) * 128] = d32[1 + u].reshape(8, K, 128).astype(BF)
@@ -220,7 +220,7 @@
     ]
 
     with scope("E_self1"):
-        lax.fori_loop(0, 3, self_part, 0, unroll=3)
+        self_part(0, 0)
 
     @pl.when(handler)
     def _():
@@ -242,13 +242,19 @@
         c_copies[0].start()
 
     with scope("F_self2"):
-        lax.fori_loop(3, 8, self_part, 0, unroll=5)
+        lax.fori_loop(1, 7, self_part, 0, unroll=6)
 
     @pl.when(handler)
     def _():
         with scope("H_wz"):
             done(g_v.at[pl.ds(0, 3)], z_r.at[1])
         c_copies[1].start()
+
+    with scope("H_self3"):
+        self_part(7, 0)
+
+    @pl.when(handler)
+    def _():
         with scope("I_wma"):
             done(m_a.at[pl.ds(0, 14)], m_r.at[0])
         with scope("I_wc"):
@@ -368,15 +374,15 @@
 
 
 def finish(acc, side_v, nbl, colb_v, dual, out, tmp, sem):
+    right = jnp.concatenate([nbl[pl.ds(0, LAST), :], dual[:, HALF:]], axis=0)
     for i in range(8):
         rows = pl.ds(i * 256, 256)
-        for u in range(2):
-            got = acc[u, rows, :] + tdot(colb_v[:, rows], dual[:, u * HALF:(u + 1) * HALF])
-            if u:
-                got = got + tdot(side_v[pl.ds(LEAF - LAST, LAST), rows], nbl[pl.ds(0, LAST), :])
-            tmp[rows, u * HALF:(u + 1) * HALF] = got
+        tmp[rows, :HALF] = acc[0, rows, :] + tdot(colb_v[:, rows], dual[:, :HALF])
+        left = jnp.concatenate([side_v[pl.ds(LEAF - LAST, LAST), rows], colb_v[:, rows]], axis=0)
+        tmp[rows, HALF:] = acc[1, rows, :] + tdot(left, right)
         pltpu.make_async_copy(tmp.at[rows], out.at[rows], sem).start()
-    pltpu.make_async_copy(tmp, out, sem).wait()
+    with scope("Z_wout"):
+        pltpu.make_async_copy(tmp, out, sem).wait()
 
 
 def on_device(*args):

time: 36.8 us -> 36.8 us (level)
  no operation moved by 1% of the time
where the time goes in v4:
time: 36.8 us; the launch traced here: 36.6 us
  Pallas kernels  35.2 us (96%)
  between operations  1.47 us (4%)
    pallas_call x1, Pallas kernels, on_device(): pl.pallas_call(kernel, out_shape=[pltpu.VMEM((2, LEAF, HALF), F32), pltpu...  32.9 us
    pallas_call x1, Pallas kernels, on_device(): pl.pallas_call(finish, out_shape=jax.ShapeDtypeStruct((LEAF, NRHS), F32),...  2.28 us

profile of v4, /device:TPU:1, one launch (start us, length us, event | category | flops | bytes accessed | tf_op | source)
XLA Modules:
  0.0 36.6 jit_solution(9278224088841350222)
XLA Ops:
  1.3 32.9 %shard_map.100 = (f32[2,2048,256]{2,1,0:T(8,128)S(1)}, bf16[2048,2048]{1,0:T(8,128)(2,1)S(1)}, bf16[512,256]{1,0:T(8,128)(2,1)S(1)}, bf16[32,2048]{1,0:T(8,128)(2,1)S(1)}, bf16[32,512]{1,0:T(8,128)(2,1)S(1)}) custom-call(bf16[2048,512]{1,0:T(8,128)(2,1)} %bitcast.19, bf16[2048,2048]{1,0:T(8,128)(2,1)} %bitcast.17, bf16[2048,2048]{1,0:T(8,128)(2,1)} %bitcast.18, ...), custom_call_target="tpu_custom_call" | custom-call | tf_op jit(solution)/shard_map/pallas_call | solution.py:400
  34.2 2.3 %shard_map.101 = f32[2048,512]{1,0:T(8,128)} custom-call(f32[2,2048,256]{2,1,0:T(8,128)S(1)} %get-tuple-element.10.acc, bf16[2048,2048]{1,0:T(8,128)(2,1)S(1)} %get-tuple-element.11.side_v, bf16[512,256]{1,0:T(8,128)(2,1)S(1)} %get-tuple-element.12.nbl, bf16[32,2048]{1,0:T(8,128)(2,1)S(1)} %get-tuple-element.13.colb_v, ...), custom_call_target="tpu_custom_call" | custom-call | tf_op jit(solution)/shard_map/pallas_call | solution.py:442

commit v5 on v4

--- a/solution.py
+++ b/solution.py
@@ -184,11 +184,17 @@
 
     @pl.when(jnp.logical_not(handler))
     def _():
-        for cp in [targ_copy] + raw_copies + [xp_copy]:
-            cp.start()
-
-    for cp in offs:
+        for cp in [xp_copy, targ_copy] + raw_copies:
+            cp.start()
+
+    for cp in offs[:8]:
         cp.start()
+
+    @pl.when(jnp.logical_not(handler))
+    def _():
+        for cp in offs[8:]:
+            cp.start()
+
     on.start()
     load_side.start()
     load_colb.start()
@@ -224,6 +230,10 @@
 
     @pl.when(handler)
     def _():
+        with scope("F_wxp"):
+            xp_copy.wait_recv()
+        for cp in z_copies[1]:
+            cp.start()
         with scope("F_wraw"):
             targ_copy.wait_recv()
             raw_copies[0].wait_recv()
@@ -231,10 +241,6 @@
             densify(raw_r, targ_r, 1, raw_copies[1].wait_recv)
         for cp in m_copies[2]:
             cp.start()
-        with scope("F_wxp"):
-            xp_copy.wait_recv()
-        for cp in z_copies[1] + m_copies[3]:
-            cp.start()
         m_a[mate] = ds_a[1, c * 4 + z]
         m_b[mate] = ds_b[1, c * 4 + z]
         with scope("F_wz"):
@@ -242,7 +248,15 @@
         c_copies[0].start()
 
     with scope("F_self2"):
-        lax.fori_loop(1, 7, self_part, 0, unroll=6)
+        lax.fori_loop(1, 4, self_part, 0, unroll=3)
+
+    @pl.when(handler)
+    def _():
+        for cp in m_copies[3]:
+            cp.start()
+
+    with scope("F_self3"):
+        lax.fori_loop(4, 7, self_part, 0, unroll=3)
 
     @pl.when(handler)
     def _():
@@ -330,6 +344,9 @@
         def _():
             for cp in far:
                 cp.start()
+
+        for cp in offs[8:]:
+            cp.start()
 
     side_part(4)
     side_part(5)

time: 36.8 us -> 36.5 us (level)
  no operation moved by 1% of the time
where the time goes in v5:
time: 36.5 us; the launch traced here: 36.4 us
  Pallas kernels  34.9 us (96%)
  between operations  1.47 us (4%)
    pallas_call x1, Pallas kernels, on_device(): pl.pallas_call(kernel, out_shape=[pltpu.VMEM((2, LEAF, HALF), F32), pltpu...  32.6 us
    pallas_call x1, Pallas kernels, on_device(): pl.pallas_call(finish, out_shape=jax.ShapeDtypeStruct((LEAF, NRHS), F32),...  2.28 us

profile of v5, /device:TPU:1, one launch (start us, length us, event | category | flops | bytes accessed | tf_op | source)
XLA Modules:
  0.0 36.4 jit_solution(14619620683379006610)
XLA Ops:
  1.3 32.6 %shard_map.100 = (f32[2,2048,256]{2,1,0:T(8,128)S(1)}, bf16[2048,2048]{1,0:T(8,128)(2,1)S(1)}, bf16[512,256]{1,0:T(8,128)(2,1)S(1)}, bf16[32,2048]{1,0:T(8,128)(2,1)S(1)}, bf16[32,512]{1,0:T(8,128)(2,1)S(1)}) custom-call(bf16[2048,512]{1,0:T(8,128)(2,1)} %bitcast.19, bf16[2048,2048]{1,0:T(8,128)(2,1)} %bitcast.17, bf16[2048,2048]{1,0:T(8,128)(2,1)} %bitcast.18, ...), custom_call_target="tpu_custom_call" | custom-call | tf_op jit(solution)/shard_map/pallas_call | solution.py:417
  33.9 2.3 %shard_map.101 = f32[2048,512]{1,0:T(8,128)} custom-call(f32[2,2048,256]{2,1,0:T(8,128)S(1)} %get-tuple-element.10.acc, bf16[2048,2048]{1,0:T(8,128)(2,1)S(1)} %get-tuple-element.11.side_v, bf16[512,256]{1,0:T(8,128)(2,1)S(1)} %get-tuple-element.12.nbl, bf16[32,2048]{1,0:T(8,128)(2,1)S(1)} %get-tuple-element.13.colb_v, ...), custom_call_target="tpu_custom_call" | custom-call | tf_op jit(solution)/shard_map/pallas_call | solution.py:459
